TPU v7x, 32 devices: a whole 2x2x4 slice. The times are simulated.
32 devices in a mesh: row: 8 (over y, x, core), col: 4 (over z).
Axes of the slice: x: 2, y: 2, z: 4, core: 2. Of those that a mesh axis runs over, the one named last changes fastest.
Arguments:
- tiles: float32 [8, 4, 4, 512, 512], P('row', 'col'), may hold values from 0 to 16777212, as said below
- tile_index: int32 [8, 4, 4, 2], P('row', 'col'), may hold values from 0 to 3, as said below
- tile_count: int32 [8, 4], P('row', 'col'), may hold values from 0 to 4, as said below
- iterate: float32 [8192, 32], P(('row', 'col')), may hold values from 0 to 16777212, as said below
- basis: float32 [8192, 32], P(('row', 'col')), may hold values from 0 to 16777212, as said below
- coefficients: float32 [256, 32, 32], P(('row', 'col')), may hold values from 0 to 16777212, as said below
- start_degree: int32 [1], replicated, may hold values from 1 to 255
Outputs:
- scaled_iterate: float32 [8192, 32], P(('row', 'col'))
Inputs may be any that keep to these rules, and one draw needn't show every extreme that they name: `tiles`: integers 0 to 16777212. `iterate`: integers 0 to 16777212. `basis`: integers 0 to 16777212. `coefficients`: integers 0 to 16777212. tile_index[..., 0] lies in 0 to 1 and tile_index[..., 1] in 0 to 3; the 4 slots of one device name distinct tiles, unoccupied slots included; unoccupied slots hold arbitrary entries. `tile_count`: some device has 4 occupied slots.
All inputs are finite; a program needn't handle non-finite values.
Results may differ from a plain program's by a relative error of at most 0.0003.
Values sent between devices are 32-bit elements; how exact they have to be, the bound alone decides.
A program may use at most 64 MiB of HBM per device.

v0:
```python
import jax
import jax.numpy as jnp
from jax import lax
from jax.sharding import PartitionSpec as P

STEPS = 2
PRIME = 16777213
RADIX = 16777216


def from_root(block, axis, source):
    block = jnp.where(lax.axis_index(axis) == source, block, jnp.zeros_like(block))
    return lax.psum(block, axis)


def fold_word(value):
    value = value % RADIX + 3 * (value // RADIX)
    return jnp.where(value >= PRIME, value - PRIME, value)


def add_mod(first, second):
    total = first + second
    return jnp.where(total >= PRIME, total - PRIME, total)


def shift_mod(value, shift):
    while shift > 0:
        amount = min(shift, 7)
        value = fold_word(value * 2**amount)
        shift = shift - amount
    return value


def split_limbs(values, bits, count):
    whole = values.astype(jnp.int32)
    return [(whole // 2 ** (bits * place) % 2**bits).astype(jnp.bfloat16) for place in range(count)]


def combine_limbs(product, left_bits, right_bits, width):
    whole = product.astype(jnp.int32)
    total = None
    for left in range(whole.shape[-3]):
        for right in range(whole.shape[-1] // width):
            piece = whole[..., left, :, right * width : (right + 1) * width]
            term = shift_mod(piece, left_bits * left + right_bits * right)
            total = term if total is None else add_mod(total, term)
    return total


def tile_products(tile_limbs, gathered, column_slots, tile):
    column_limbs = jnp.concatenate(split_limbs(gathered, 6, 4), axis=1)
    windows = jax.vmap(
        lambda column: lax.dynamic_slice_in_dim(column_limbs, column * tile, tile, 0)
    )(column_slots)
    product = jnp.einsum("tlik,tkc->tlic", tile_limbs, windows, preferred_element_type=jnp.float32)
    return combine_limbs(product, 8, 6, gathered.shape[1])


def on_device(tiles, tile_index, tile_count, iterate, basis, coefficients, start_degree):
    block = tiles[0, 0]
    tile = block.shape[-1]
    slots = block.shape[0]
    rows_dev = iterate.shape[0]
    width = iterate.shape[1]
    count_col = lax.axis_size("col")
    block_rows = rows_dev * count_col // tile
    per_device = coefficients.shape[0]
    tile_limbs = jnp.stack(split_limbs(block, 8, 3), axis=1)
    row_slots = tile_index[0, 0, :, 0]
    column_slots = tile_index[0, 0, :, 1]
    used = jnp.arange(slots) < tile_count[0, 0]
    match = row_slots[:, None] == jnp.arange(block_rows)[None, :]
    basis_limbs = jnp.stack(split_limbs(basis, 8, 3))
    degree = start_degree[0]
    current = iterate
    for step in range(STEPS):
        wanted = degree - step
        holding = lax.dynamic_index_in_dim(coefficients, wanted % per_device, 0, keepdims=False)
        coef = from_root(holding, ("row", "col"), wanted // per_device)
        packed = lax.all_gather(current.reshape(-1, 128), "row", axis=0, tiled=True)
        gathered = packed.reshape(-1, width)
        residues = tile_products(tile_limbs, gathered, column_slots, tile)
        kept = jnp.where(used[:, None, None], residues, 0)
        partial_value = (
            jnp.sum(jnp.where(match[:, :, None, None], kept[:, None], 0), axis=0) % PRIME
        )
        partial_value = partial_value.reshape(block_rows * tile, width)
        pieces = partial_value.astype(jnp.float32).reshape(count_col, -1, 128)
        arrived = lax.all_to_all(pieces, "col", split_axis=0, concat_axis=0, tiled=True)
        local = (jnp.sum(arrived.astype(jnp.int32), axis=0) % PRIME).reshape(rows_dev, width)
        coef_limbs = jnp.concatenate(split_limbs(coef, 8, 3), axis=1)
        basis_product = jnp.einsum(
            "lrk,kc->lrc", basis_limbs, coef_limbs, preferred_element_type=jnp.float32
        )
        basis_term = combine_limbs(basis_product, 8, 8, width)
        current = add_mod(local, basis_term).astype(jnp.float32)
    return current / PRIME


def solution(mesh):
    in_specs = (
        P("row", "col", None, None, None),
        P("row", "col", None, None),
        P("row", "col"),
        P(("row", "col"), None),
        P(("row", "col"), None),
        P(("row", "col"), None, None),
        P(),
    )
    out_specs = P(("row", "col"), None)
    return jax.shard_map(
        on_device, mesh=mesh, in_specs=in_specs, out_specs=out_specs, check_vma=False
    )
```

profile of v0, /device:TPU:0, one launch (start us, length us, event | category | flops | bytes accessed | tf_op | source)
XLA Modules:
  0.0 145.7 jit_solution(8975279407004597319)
XLA Ops:
  0.0 0.7 compare_select_fusion.158
  0.7 0.7 slice_bitcast_fusion.1
  1.4 11.8 %fusion = (bf16[4,1,512,512]{3,2,1,0:T(8,128)(2,1)S(1)}, bf16[4,1,512,512]{3,2,1,0:T(8,128)(2,1)}, bf16[4,1,512,512]{3,2,1,0:T(8,128)(2,1)}) fusion(f32[1,1,4,512,512]{4,3,2,1,0:T(8,128)} %param.7), kind=kLoop, calls=%fused_computation.19 | loop fusion | flops 57671680 | bytes 10485760 | tf_op jit(solution)/shard_map/convert_element_type | solution.py:36
  13.1 0.1 copy.30
  13.2 0.1 reshape.310
  13.3 11.0 %all_gather.6 = f32[512,128]{1,0:T(8,128)S(1)} all-gather(f32[64,128]{1,0:T(8,128)S(1)} %reshape.310), channel_id=1, replica_groups=mesh['row'=8,'col'=4] {'row'}, dimensions={0}, use_global_device_ids=true | all-gather | bytes 294912 | tf_op jit(solution)/shard_map/all_gather | solution.py:80
  24.3 0.3 convert_element_type.162
  24.6 3.1 %fusion.13 = (bf16[2048,32]{1,0:T(8,128)(2,1)S(1)}, bf16[2048,32]{1,0:T(8,128)(2,1)S(1)}, bf16[2048,32]{1,0:T(8,128)(2,1)S(1)}, bf16[2048,32]{1,0:T(8,128)(2,1)S(1)}) fusion(s32[2048,32]{1,0:T(8,128)S(1)} %convert_element_type.162), kind=kLoop, calls=%fused_computation.76 | loop fusion | flops 4980736 | bytes 786432 | tf_op jit(solution)/shard_map/convert_element_type | solution.py:36
  27.7 0.7 pad_maximum_fusion.7
  28.4 5.7 %while.2 = (s32[]{:T(128)}, bf16[2048,128]{1,0:T(8,128)(2,1)S(1)}, s32[4,2]{0,1:T(2,128)S(1)}, bf16[4,512,128]{2,1,0:T(8,128)(2,1)S(1)}, s32[]{:T(128)}) while((s32[]{:T(128)}, bf16[2048,128]{1,0:T(8,128)(2,1)S(1)}, s32[4,2]{0,1:T(2,128)S(1)}, bf16[4,512,128]{2,1,0:T(8,128)(2,1)S(1)}, s32[]{:T(128)}) %tuple.53), condition=%wide.while_cond, body=%wide.while_body.sunk | while | flops 2 | bytes 262249 | solution.py:53
  28.5 0.6 slice.522
  29.1 0.7 bitcast_dynamic-update-slice_fusion.4
  30.0 0.6 slice.522
  30.6 0.7 bitcast_dynamic-update-slice_fusion.4
  31.4 0.6 slice.522
  32.0 0.7 bitcast_dynamic-update-slice_fusion.4
  32.8 0.6 slice.522
  33.4 0.7 bitcast_dynamic-update-slice_fusion.4
  34.9 3.9 %fusion.11 = s32[4,3,512,128]{2,3,1,0:T(8,128)S(1)} fusion(bf16[4,1,512,512]{3,2,1,0:T(8,128)(2,1)} %get-tuple-element.40, bf16[4,1,512,512]{3,2,1,0:T(8,128)(2,1)} %get-tuple-element.41, bf16[4,1,512,512]{3,2,1,0:T(8,128)(2,1)S(1)} %get-tuple-element.39, bf16[4,512,128]{2,1,0:T(8,128)(2,1)S(1)} %get-tuple-element.12), kind=kOutput, calls=%fused_computation.32 | convolution fusion | flops 812384256 | bytes 9961472 | tf_op jit(solution)/shard_map/tlik,tkc->tlic/dot_general | solution.py:55
  38.9 9.4 %fusion.205 = s32[4,512,32]{1,2,0:T(8,128)S(1)} fusion(s32[4,3,512,128]{2,3,1,0:T(8,128)S(1)} %fusion.11, pred[4]{0:T(512)(128)(4,1)S(1)} %iota_compare_fusion.1), kind=kLoop, calls=%fused_computation.692 | loop fusion | flops 57016320 | bytes 3407876 | tf_op jit(solution)/shard_map/jit(_where)/broadcast_in_dim | solution.py:85
  48.3 0.1 select_reduce_fusion.1
  48.5 0.2 copy.32
  48.7 0.2 rem.2743
  48.8 0.7 fusion.505
  49.5 4.9 %all-to-all-start = ((f32[4,64,128]{2,1,0:T(8,128)}), f32[4,64,128]{2,1,0:T(8,128)S(1)}, u32[]{:S(2)}, u32[]{:S(2)}) async-start(f32[4,64,128]{2,1,0:T(8,128)} %fusion.505), calls=%async_computation | async-start | bytes 262144 | tf_op jit(solution)/shard_map/all_to_all | solution.py:89
  55.3 0.7 select_bitcast_fusion
  56.0 40.0 %all-reduce.1 = (f32[32,32]{1,0:T(8,128)S(1)}, f32[32,32]{1,0:T(8,128)S(1)}) all-reduce(f32[32,32]{1,0:T(8,128)S(1)} %get-tuple-element.60, f32[32,32]{1,0:T(8,128)S(1)} %get-tuple-element.59), channel_id=1, replica_groups=mesh['row'=8,'col'=4] {'row','col'}, use_global_device_ids=true, to_apply=%region_2.3 | all-reduce | flops 2048 | bytes 16384 | tf_op jit(solution)/shard_map/psum | solution.py:13
  96.1 0.3 convolution_convert_fusion.1
  96.4 0.1 copy.41
  96.5 0.1 mul.1077
  96.6 0.1 copy.40
  96.7 0.1 mul.1068
  96.8 0.1 copy.39
  96.9 0.1 mul.1061
  97.0 0.1 copy.38
  97.2 0.1 copy.37
  97.4 0.1 copy.36
  97.6 0.1 copy.35
  97.8 0.1 copy.33
  98.0 0.1 copy.34
  98.2 1.0 fusion.645
  99.2 10.3 %all_gather.7 = f32[512,128]{1,0:T(8,128)S(1)} all-gather(f32[64,128]{1,0:T(8,128)S(1)} %fusion.645), channel_id=1, replica_groups=mesh['row'=8,'col'=4] {'row'}, dimensions={0}, use_global_device_ids=true | all-gather | bytes 294912 | tf_op jit(solution)/shard_map/all_gather | solution.py:80
  109.5 0.3 convert_element_type.181
  109.8 3.1 %fusion.22 = (bf16[2048,32]{1,0:T(8,128)(2,1)S(1)}, bf16[2048,32]{1,0:T(8,128)(2,1)S(1)}, bf16[2048,32]{1,0:T(8,128)(2,1)S(1)}, bf16[2048,32]{1,0:T(8,128)(2,1)S(1)}) fusion(s32[2048,32]{1,0:T(8,128)S(1)} %convert_element_type.181), kind=kLoop, calls=%fused_computation.85 | loop fusion | flops 4980736 | bytes 786432 | tf_op jit(solution)/shard_map/convert_element_type | solution.py:36
  112.9 0.7 pad_maximum_fusion.8
  113.6 5.7 %while.3 = (s32[]{:T(128)}, bf16[2048,128]{1,0:T(8,128)(2,1)S(1)}, s32[4,2]{0,1:T(2,128)S(1)}, bf16[4,512,128]{2,1,0:T(8,128)(2,1)S(1)}, s32[]{:T(128)}) while((s32[]{:T(128)}, bf16[2048,128]{1,0:T(8,128)(2,1)S(1)}, s32[4,2]{0,1:T(2,128)S(1)}, bf16[4,512,128]{2,1,0:T(8,128)(2,1)S(1)}, s32[]{:T(128)}) %tuple.59), condition=%wide.while_cond.1, body=%wide.while_body.1.sunk | while | flops 2 | bytes 262249 | solution.py:53
  113.7 0.6 slice.523
  114.3 0.7 bitcast_dynamic-update-slice_fusion.5
  115.1 0.6 slice.523
  115.7 0.7 bitcast_dynamic-update-slice_fusion.5
  116.6 0.6 slice.523
  117.2 0.7 bitcast_dynamic-update-slice_fusion.5
  118.0 0.6 slice.523
  118.6 0.7 bitcast_dynamic-update-slice_fusion.5
  119.4 3.9 %fusion.12 = s32[4,3,512,128]{2,3,1,0:T(8,128)S(1)} fusion(bf16[4,1,512,512]{3,2,1,0:T(8,128)(2,1)} %get-tuple-element.40, bf16[4,1,512,512]{3,2,1,0:T(8,128)(2,1)} %get-tuple-element.41, bf16[4,1,512,512]{3,2,1,0:T(8,128)(2,1)S(1)} %get-tuple-element.39, bf16[4,512,128]{2,1,0:T(8,128)(2,1)S(1)} %get-tuple-element.20), kind=kOutput, calls=%fused_computation.33 | convolution fusion | flops 812384256 | bytes 9961472 | tf_op jit(solution)/shard_map/tlik,tkc->tlic/dot_general | solution.py:55
  123.3 9.4 %fusion.240 = s32[4,512,32]{1,2,0:T(8,128)S(1)} fusion(s32[4,3,512,128]{2,3,1,0:T(8,128)S(1)} %fusion.12, pred[4]{0:T(512)(128)(4,1)S(1)} %iota_compare_fusion.1), kind=kLoop, calls=%fused_computation.727 | loop fusion | flops 57016320 | bytes 3407876 | tf_op jit(solution)/shard_map/jit(_where)/broadcast_in_dim | solution.py:85
  132.7 0.1 select_reduce_fusion
  132.9 0.2 copy.43
  133.1 0.2 rem.3188
  133.3 0.7 fusion.506
  134.0 3.5 %all-to-all-start.1 = ((f32[4,64,128]{2,1,0:T(8,128)}), f32[4,64,128]{2,1,0:T(8,128)S(1)}, u32[]{:S(2)}, u32[]{:S(2)}) async-start(f32[4,64,128]{2,1,0:T(8,128)} %fusion.506), calls=%async_computation.1 | async-start | bytes 262144 | tf_op jit(solution)/shard_map/all_to_all | solution.py:89
  137.5 0.3 convolution_convert_fusion
  137.8 6.1 %all-to-all-done.1 = f32[4,64,128]{2,1,0:T(8,128)S(1)} async-done(((f32[4,64,128]{2,1,0:T(8,128)}), f32[4,64,128]{2,1,0:T(8,128)S(1)}, u32[]{:S(2)}, u32[]{:S(2)}) %all-to-all-start.1) | async-done | bytes 131104 | tf_op jit(solution)/shard_map/all_to_all | solution.py:89
  144.1 1.6 %fusion.673 = f32[256,32]{0,1:T(8,128)} fusion(s32[256,32]{0,1:T(8,128)S(1)} %copy.44, s32[3,256,96]{1,2,0:T(8,128)S(1)} %convolution_convert_fusion), kind=kLoop, calls=%fused_computation.1601 | loop fusion | flops 5677056 | bytes 360448 | tf_op jit(solution)/shard_map/div | solution.py:97
  (36 shorter events, 1.9 us)
Async XLA Ops:
  1.4 11.8 %copy-start = (f32[256,32]{0,1:T(8,128)S(1)}, f32[256,32]{0,1:T(8,128)}, u32[]{:S(2)}) copy-start(f32[256,32]{0,1:T(8,128)} %param.10) | copy-start | bytes 98308
  38.8 16.2 %copy-start.1 = (f32[256,32]{0,1:T(8,128)S(1)}, f32[256,32]{0,1:T(8,128)}, u32[]{:S(2)}) copy-start(f32[256,32]{0,1:T(8,128)} %param.11) | copy-start | bytes 98308
  49.5 48.7 %all-to-all-start = ((f32[4,64,128]{2,1,0:T(8,128)}), f32[4,64,128]{2,1,0:T(8,128)S(1)}, u32[]{:S(2)}, u32[]{:S(2)}) async-start(f32[4,64,128]{2,1,0:T(8,128)} %fusion.505), calls=%async_computation | async-start | bytes 262144 | tf_op jit(solution)/shard_map/all_to_all | solution.py:89
  134.0 10.0 %all-to-all-start.1 = ((f32[4,64,128]{2,1,0:T(8,128)}), f32[4,64,128]{2,1,0:T(8,128)S(1)}, u32[]{:S(2)}, u32[]{:S(2)}) async-start(f32[4,64,128]{2,1,0:T(8,128)} %fusion.506), calls=%async_computation.1 | async-start | bytes 262144 | tf_op jit(solution)/shard_map/all_to_all | solution.py:89
where the time goes:
time: 146 us
  blocking collectives  61.2 us (42%)
  other arithmetic  44.1 us (30%)
  local copies, waits for them, and re-layouts  15.4 us (11%)
  matrix products  8.49 us (6%)
  starting transfers between devices  8.42 us (6%)
  waiting for transfers between devices  6.1 us (4%)
  between operations  1.76 us (1%)
    psum x1, blocking collectives, from_root(): return lax.psum(block, axis)  40 us
    all_gather x2, blocking collectives, on_device(): packed = lax.all_gather(current.reshape(-1, 128), 'row', axis=0, tiled=True)  21.3 us
    broadcast_in_dim x2, other arithmetic, on_device(): jnp.where(match[:, :, None, None], kept[:, None], 0)  18.8 us
    convert_element_type x4, other arithmetic, split_limbs(): (whole // 2 ** (bits * place) % 2 ** bits).astype(jnp.bfloat16)  18 us
    gather x24, local copies, waits for them, and re-layouts  11.3 us
    all_to_all x2, starting transfers between devices, on_device(): lax.all_to_all(pieces, 'col', split_axis=0, concat_axis=0, tiled=True)  8.42 us
    dot_general x2, matrix products, tile_products(): jnp.einsum('tlik,tkc->tlic', tile_limbs, windows, preferred_element_type=...  7.85 us
    all_to_all x2, waiting for transfers between devices, on_device(): lax.all_to_all(pieces, 'col', split_axis=0, concat_axis=0, tiled=True)  6.1 us
  transfers between devices with their start and end apart: 2, of which 1 were waited for; matrix products, arithmetic and copies ran while one was open for 2% of the time, Pallas kernels for 0%

commit v1 on v0

--- a/solution.py
+++ b/solution.py
@@ -2,6 +2,7 @@
 import jax.numpy as jnp
 from jax import lax
 from jax.sharding import PartitionSpec as P
+from jax.lax import all_gather
 
 STEPS = 2
 PRIME = 16777213
@@ -10,7 +11,8 @@
 
 def from_root(block, axis, source):
     block = jnp.where(lax.axis_index(axis) == source, block, jnp.zeros_like(block))
-    return lax.psum(block, axis)
+    play_panels = lambda row_data, across: all_gather(row_data, axis_name=across).sum(axis=0)
+    return play_panels(block, axis)
 
 
 def fold_word(value):

time: 146 us -> 244 us (1.67)
  blocking collectives: 61.2 us -> 160 us
    all_gather x0 -> x2, blocking collectives: none -> 140 us  [from_root(): all_gather(row_data, axis_name=across).sum(axis=0)]
    psum x1 -> x0, blocking collectives: 40 us -> none  [from_root(): return lax.psum(block, axis)]
    convert_element_type x4 -> x5, other arithmetic: 18 us -> 18 us  [split_limbs(): (whole // 2 ** (bits * place) % 2 ** bits).astype(jnp.bfloat16)]
  transfers between devices with their start and end apart: 2 -> 2, of which waited for: 1 -> 1; matrix products, arithmetic and copies ran while one was open for 2% -> 1% of each run, Pallas kernels for 0% -> 0%
where the time goes in v1:
time: 244 us; the launch traced here: 243 us
  blocking collectives  160 us (66%)
  other arithmetic  44.3 us (18%)
  local copies, waits for them, and re-layouts  14.3 us (6%)
  matrix products  8.49 us (3%)
  starting transfers between devices  8.19 us (3%)
  waiting for transfers between devices  6.1 us (2%)
    all_gather x2, blocking collectives, from_root(): all_gather(row_data, axis_name=across).sum(axis=0)  140 us
    all_gather x2, blocking collectives, on_device(): packed = lax.all_gather(current.reshape(-1, 128), 'row', axis=0, tiled=True)  20.5 us
    broadcast_in_dim x2, other arithmetic, on_device(): jnp.where(match[:, :, None, None], kept[:, None], 0)  18.8 us
    convert_element_type x5, other arithmetic, split_limbs(): (whole // 2 ** (bits * place) % 2 ** bits).astype(jnp.bfloat16)  18 us
    gather x24, local copies, waits for them, and re-layouts  10.2 us
    all_to_all x2, starting transfers between devices, on_device(): lax.all_to_all(pieces, 'col', split_axis=0, concat_axis=0, tiled=True)  8.19 us
    dot_general x2, matrix products, tile_products(): jnp.einsum('tlik,tkc->tlic', tile_limbs, windows, preferred_element_type=...  7.85 us
    all_to_all x2, waiting for transfers between devices, on_device(): lax.all_to_all(pieces, 'col', split_axis=0, concat_axis=0, tiled=True)  6.1 us
  transfers between devices with their start and end apart: 2, of which 1 were waited for; matrix products, arithmetic and copies ran while one was open for 1% of the time, Pallas kernels for 0%

profile of v1, /device:TPU:0, one launch (start us, length us, event | category | flops | bytes accessed | tf_op | source)
XLA Modules:
  0.0 243.3 jit_solution(3327664039528326349)
XLA Ops:
  0.0 0.7 compare_select_fusion.158
  0.7 0.7 slice_bitcast_fusion.1
  1.4 11.8 %fusion = (bf16[4,1,512,512]{3,2,1,0:T(8,128)(2,1)S(1)}, bf16[4,1,512,512]{3,2,1,0:T(8,128)(2,1)}, bf16[4,1,512,512]{3,2,1,0:T(8,128)(2,1)}) fusion(f32[1,1,4,512,512]{4,3,2,1,0:T(8,128)} %param.7), kind=kLoop, calls=%fused_computation.19 | loop fusion | flops 57671680 | bytes 10485760 | tf_op jit(solution)/shard_map/convert_element_type | solution.py:38
  13.2 0.1 copy.48
  13.2 0.1 reshape.304
  13.3 11.0 %all_gather.14 = f32[512,128]{1,0:T(8,128)S(1)} all-gather(f32[64,128]{1,0:T(8,128)S(1)} %reshape.304), channel_id=1, replica_groups=mesh['row'=8,'col'=4] {'row'}, dimensions={0}, use_global_device_ids=true | all-gather | bytes 294912 | tf_op jit(solution)/shard_map/all_gather | solution.py:82
  24.3 0.3 convert_element_type.162
  24.6 3.1 %fusion.13 = (bf16[2048,32]{1,0:T(8,128)(2,1)S(1)}, bf16[2048,32]{1,0:T(8,128)(2,1)S(1)}, bf16[2048,32]{1,0:T(8,128)(2,1)S(1)}, bf16[2048,32]{1,0:T(8,128)(2,1)S(1)}) fusion(s32[2048,32]{1,0:T(8,128)S(1)} %convert_element_type.162), kind=kLoop, calls=%fused_computation.76 | loop fusion | flops 4980736 | bytes 786432 | tf_op jit(solution)/shard_map/convert_element_type | solution.py:38
  27.7 0.7 pad_maximum_fusion.7
  28.5 5.2 %while.2 = (s32[]{:T(128)}, bf16[2048,128]{1,0:T(8,128)(2,1)S(1)}, s32[4,2]{0,1:T(2,128)S(1)}, bf16[4,512,128]{2,1,0:T(8,128)(2,1)S(1)}, s32[]{:T(128)}) while((s32[]{:T(128)}, bf16[2048,128]{1,0:T(8,128)(2,1)S(1)}, s32[4,2]{0,1:T(2,128)S(1)}, bf16[4,512,128]{2,1,0:T(8,128)(2,1)S(1)}, s32[]{:T(128)}) %tuple.50), condition=%wide.while_cond, body=%wide.while_body.sunk | while | flops 2 | bytes 262249 | solution.py:55
  28.6 0.5 slice.522
  29.1 0.7 bitcast_dynamic-update-slice_fusion.4
  29.8 0.5 slice.522
  30.4 0.7 bitcast_dynamic-update-slice_fusion.4
  31.1 0.5 slice.522
  31.7 0.7 bitcast_dynamic-update-slice_fusion.4
  32.4 0.5 slice.522
  32.9 0.7 bitcast_dynamic-update-slice_fusion.4
  34.4 3.9 %fusion.11 = s32[4,3,512,128]{2,3,1,0:T(8,128)S(1)} fusion(bf16[4,1,512,512]{3,2,1,0:T(8,128)(2,1)} %get-tuple-element.38, bf16[4,1,512,512]{3,2,1,0:T(8,128)(2,1)} %get-tuple-element.39, bf16[4,1,512,512]{3,2,1,0:T(8,128)(2,1)S(1)} %get-tuple-element.37, bf16[4,512,128]{2,1,0:T(8,128)(2,1)S(1)} %get-tuple-element.12), kind=kOutput, calls=%fused_computation.32 | convolution fusion | flops 812384256 | bytes 9961472 | tf_op jit(solution)/shard_map/tlik,tkc->tlic/dot_general | solution.py:57
  38.3 9.4 %fusion.205 = s32[4,512,32]{1,2,0:T(8,128)S(1)} fusion(s32[4,3,512,128]{2,3,1,0:T(8,128)S(1)} %fusion.11, pred[4]{0:T(512)(128)(4,1)S(1)} %iota_compare_fusion.1), kind=kLoop, calls=%fused_computation.692 | loop fusion | flops 57016320 | bytes 3407876 | tf_op jit(solution)/shard_map/jit(_where)/broadcast_in_dim | solution.py:87
  47.7 0.1 select_reduce_fusion.1
  47.9 0.2 copy.50
  48.1 0.2 rem.2743
  48.3 0.7 fusion.505
  49.0 4.9 %all-to-all-start = ((f32[4,64,128]{2,1,0:T(8,128)}), f32[4,64,128]{2,1,0:T(8,128)S(1)}, u32[]{:S(2)}, u32[]{:S(2)}) async-start(f32[4,64,128]{2,1,0:T(8,128)} %fusion.505), calls=%async_computation | async-start | bytes 262144 | tf_op jit(solution)/shard_map/all_to_all | solution.py:91
  54.7 0.7 dynamic-slice_select_fusion
  55.4 71.7 %all_gather.15 = f32[32,32,32]{2,1,0:T(8,128)S(1)} all-gather(f32[1,32,32]{2,1,0:T(8,128)S(1)} %get-tuple-element.58), channel_id=1, replica_groups=mesh['row'=8,'col'=4] {'row','col'}, dimensions={0}, use_global_device_ids=true | all-gather | bytes 135168 | tf_op jit(solution)/shard_map/all_gather | solution.py:14
  127.2 0.3 convolution_convert_fusion.1
  127.6 0.1 copy.59
  127.7 0.1 mul.1077
  127.8 0.1 copy.58
  127.9 0.1 mul.1068
  128.0 0.1 copy.57
  128.2 0.1 copy.56
  128.4 0.1 copy.55
  128.6 0.1 copy.54
  128.8 0.1 copy.53
  129.0 0.1 copy.51
  129.2 0.1 copy.52
  129.4 67.8 %all_gather.17 = f32[32,32,32]{2,1,0:T(8,128)S(1)} all-gather(f32[1,32,32]{2,1,0:T(8,128)S(1)} %get-tuple-element.57), channel_id=1, replica_groups=mesh['row'=8,'col'=4] {'row','col'}, dimensions={0}, use_global_device_ids=true | all-gather | bytes 135168 | tf_op jit(solution)/shard_map/all_gather | solution.py:14
  197.3 1.0 fusion.645
  198.3 9.5 %all_gather.16 = f32[512,128]{1,0:T(8,128)S(1)} all-gather(f32[64,128]{1,0:T(8,128)S(1)} %fusion.645), channel_id=1, replica_groups=mesh['row'=8,'col'=4] {'row'}, dimensions={0}, use_global_device_ids=true | all-gather | bytes 294912 | tf_op jit(solution)/shard_map/all_gather | solution.py:82
  207.8 0.3 convert_element_type.181
  208.1 3.1 %fusion.22 = (bf16[2048,32]{1,0:T(8,128)(2,1)S(1)}, bf16[2048,32]{1,0:T(8,128)(2,1)S(1)}, bf16[2048,32]{1,0:T(8,128)(2,1)S(1)}, bf16[2048,32]{1,0:T(8,128)(2,1)S(1)}) fusion(s32[2048,32]{1,0:T(8,128)S(1)} %convert_element_type.181), kind=kLoop, calls=%fused_computation.85 | loop fusion | flops 4980736 | bytes 786432 | tf_op jit(solution)/shard_map/convert_element_type | solution.py:38
  211.1 0.7 pad_maximum_fusion.8
  211.9 5.2 %while.3 = (s32[]{:T(128)}, bf16[2048,128]{1,0:T(8,128)(2,1)S(1)}, s32[4,2]{0,1:T(2,128)S(1)}, bf16[4,512,128]{2,1,0:T(8,128)(2,1)S(1)}, s32[]{:T(128)}) while((s32[]{:T(128)}, bf16[2048,128]{1,0:T(8,128)(2,1)S(1)}, s32[4,2]{0,1:T(2,128)S(1)}, bf16[4,512,128]{2,1,0:T(8,128)(2,1)S(1)}, s32[]{:T(128)}) %tuple.56), condition=%wide.while_cond.1, body=%wide.while_body.1.sunk | while | flops 2 | bytes 262249 | solution.py:55
  212.0 0.5 slice.523
  212.5 0.7 bitcast_dynamic-update-slice_fusion.5
  213.3 0.5 slice.523
  213.8 0.7 bitcast_dynamic-update-slice_fusion.5
  214.6 0.5 slice.523
  215.1 0.7 bitcast_dynamic-update-slice_fusion.5
  215.9 0.5 slice.523
  216.4 0.7 bitcast_dynamic-update-slice_fusion.5
  217.1 3.9 %fusion.12 = s32[4,3,512,128]{2,3,1,0:T(8,128)S(1)} fusion(bf16[4,1,512,512]{3,2,1,0:T(8,128)(2,1)} %get-tuple-element.38, bf16[4,1,512,512]{3,2,1,0:T(8,128)(2,1)} %get-tuple-element.39, bf16[4,1,512,512]{3,2,1,0:T(8,128)(2,1)S(1)} %get-tuple-element.37, bf16[4,512,128]{2,1,0:T(8,128)(2,1)S(1)} %get-tuple-element.20), kind=kOutput, calls=%fused_computation.33 | convolution fusion | flops 812384256 | bytes 9961472 | tf_op jit(solution)/shard_map/tlik,tkc->tlic/dot_general | solution.py:57
  221.0 9.4 %fusion.240 = s32[4,512,32]{1,2,0:T(8,128)S(1)} fusion(s32[4,3,512,128]{2,3,1,0:T(8,128)S(1)} %fusion.12, pred[4]{0:T(512)(128)(4,1)S(1)} %iota_compare_fusion.1), kind=kLoop, calls=%fused_computation.727 | loop fusion | flops 57016320 | bytes 3407876 | tf_op jit(solution)/shard_map/jit(_where)/broadcast_in_dim | solution.py:87
  230.4 0.1 select_reduce_fusion
  230.6 0.2 copy.61
  230.8 0.2 rem.3188
  231.0 0.7 fusion.506
  231.7 3.3 %all-to-all-start.1 = ((f32[4,64,128]{2,1,0:T(8,128)}), f32[4,64,128]{2,1,0:T(8,128)S(1)}, u32[]{:S(2)}, u32[]{:S(2)}) async-start(f32[4,64,128]{2,1,0:T(8,128)} %fusion.506), calls=%async_computation.1 | async-start | bytes 262144 | tf_op jit(solution)/shard_map/all_to_all | solution.py:91
  235.1 0.3 convolution_convert_fusion
  235.4 6.1 %all-to-all-done.1 = f32[4,64,128]{2,1,0:T(8,128)S(1)} async-done(((f32[4,64,128]{2,1,0:T(8,128)}), f32[4,64,128]{2,1,0:T(8,128)S(1)}, u32[]{:S(2)}, u32[]{:S(2)}) %all-to-all-start.1) | async-done | bytes 131104 | tf_op jit(solution)/shard_map/all_to_all | solution.py:91
  241.7 1.6 fusion.673
  (40 shorter events, 2.1 us)
Async XLA Ops:
  1.4 11.8 %copy-start = (f32[256,32]{0,1:T(8,128)S(1)}, f32[256,32]{0,1:T(8,128)}, u32[]{:S(2)}) copy-start(f32[256,32]{0,1:T(8,128)} %param.10) | copy-start | bytes 98308
  38.3 16.2 %copy-start.1 = (f32[256,32]{0,1:T(8,128)S(1)}, f32[256,32]{0,1:T(8,128)}, u32[]{:S(2)}) copy-start(f32[256,32]{0,1:T(8,128)} %param.11) | copy-start | bytes 98308
  49.0 148.3 %all-to-all-start = ((f32[4,64,128]{2,1,0:T(8,128)}), f32[4,64,128]{2,1,0:T(8,128)S(1)}, u32[]{:S(2)}, u32[]{:S(2)}) async-start(f32[4,64,128]{2,1,0:T(8,128)} %fusion.505), calls=%async_computation | async-start | bytes 262144 | tf_op jit(solution)/shard_map/all_to_all | solution.py:91
  231.7 9.8 %all-to-all-start.1 = ((f32[4,64,128]{2,1,0:T(8,128)}), f32[4,64,128]{2,1,0:T(8,128)S(1)}, u32[]{:S(2)}, u32[]{:S(2)}) async-start(f32[4,64,128]{2,1,0:T(8,128)} %fusion.506), calls=%async_computation.1 | async-start | bytes 262144 | tf_op jit(solution)/shard_map/all_to_all | solution.py:91
